TPU v7x, 32 devices: a whole 2x2x4 slice. The times are simulated.
32 devices in a mesh: beam: 2 (over y), tm: 4 (over x, core), dm: 4 (over z).
Axes of the slice: x: 2, y: 2, z: 4, core: 2. Of those that a mesh axis runs over, the one named last changes fastest.
Arguments:
- series: float32 [16, 524288], P(('beam', 'dm'), 'tm'), parts along dimension 0, may hold values from -16 to 16
- cand_start: int32 [8, 4, 4, 16], P(('beam', 'tm'), 'dm'), parts along dimension 0, may hold values from 0 to 8064
- cand_count: int32 [8, 4, 4], P(('beam', 'tm'), 'dm'), parts along dimension 0, may hold values from 0 to 16, as said below
Outputs:
- harmonic_sum: float32 [16, 32768], P(('beam', 'dm'), 'tm'), parts along dimension 0
- sifted: float32 [8, 4, 4, 16, 128], P(('beam', 'tm'), 'dm'), parts along dimension 0
There are 2 independent parts, one for each index of `beam`. A program takes and returns all parts, laid end to end along the dimension named above; each array names one. Nothing has to cross between parts.
Inputs may be any that keep to these rules, and one draw needn't show every extreme that they name: `cand_count`: in every draw some destination band receives 16 live slots from every source band and frequency shard.
All inputs are finite; a program needn't handle non-finite values.
Results may differ from a plain program's by a relative error of at most 0.00015.
Values sent between devices are 32-bit elements; how exact they have to be, the bound alone decides.
A program may use at most 128 MiB of HBM per device.

v0:
```python
import math

import jax
import jax.numpy as jnp
import numpy as np
from jax import lax
from jax.sharding import PartitionSpec as P

NT = 524288
N1 = 512
HARM = 8
BW = 128


EPSILON = 1e-06


def contract(pattern, left, right):
    return jnp.einsum(pattern, left, right, precision=lax.Precision.HIGHEST)


def phase_table(left, right, period):
    turns = left[:, None] * right[None, :] % period
    angle = turns.astype(jnp.float32) * (2.0 * math.pi / period)
    return (jnp.cos(angle), jnp.sin(angle))


def twist(real_part, imag_part, cos_twist, sin_twist):
    return (
        real_part * cos_twist + imag_part * sin_twist,
        imag_part * cos_twist - real_part * sin_twist,
    )


def locate_column(column, per_shard):
    return (column // per_shard, column % per_shard)


def harmonic_tables(column_count, shards, per_shard, harmonics):
    listing = [[[] for harmonic in range(harmonics)] for holder in range(shards)]
    for harmonic in range(1, harmonics + 1):
        for residue in range(column_count):
            product = harmonic * residue
            holder, position = locate_column(product % column_count, per_shard)
            listing[holder][harmonic - 1].append((residue, position, product // column_count))
    slot_width = max((max((len(entries) for entries in group)) for group in listing))
    residue_tab = np.zeros((shards, harmonics, slot_width), np.int32)
    position_tab = np.zeros((shards, harmonics, slot_width), np.int32)
    base_tab = np.zeros((shards, harmonics, slot_width), np.int32)
    valid_tab = np.zeros((shards, harmonics, slot_width), np.float32)
    for holder in range(shards):
        for index in range(harmonics):
            for slot, entry in enumerate(listing[holder][index]):
                residue_tab[holder, index, slot] = entry[0]
                position_tab[holder, index, slot] = entry[1]
                base_tab[holder, index, slot] = entry[2]
                valid_tab[holder, index, slot] = 1.0
    return (residue_tab, position_tab, base_tab, valid_tab)


def per_device(series, cand_start, cand_count):
    dm_rows, samples_dev = series.shape
    shards = lax.axis_size("tm")
    my_index = lax.axis_index("tm")
    inner_len = NT // N1
    kept_bins = inner_len // 2
    per_shard = N1 // shards
    columns = jnp.arange(N1, dtype=jnp.int32)
    coarse_rows = samples_dev // inner_len
    rows_local = series.reshape(dm_rows, coarse_rows, inner_len)
    cos_first, sin_first = phase_table(columns, columns, N1)
    narrow = inner_len // shards
    inner_ids = my_index * narrow + jnp.arange(narrow, dtype=jnp.int32)
    cos_twist, sin_twist = phase_table(inner_ids, columns, NT)
    samples = lax.all_to_all(rows_local, "tm", split_axis=2, concat_axis=1, tiled=True)
    real_part = contract("nab,ar->nbr", samples, cos_first)
    imag_part = -contract("nab,ar->nbr", samples, sin_first)
    twist_re, twist_im = twist(real_part, imag_part, cos_twist, sin_twist)
    cos_second, sin_second = phase_table(
        jnp.arange(inner_len, dtype=jnp.int32), jnp.arange(kept_bins, dtype=jnp.int32), inner_len
    )
    part_re = lax.all_to_all(twist_re, "tm", split_axis=2, concat_axis=1, tiled=True)
    part_im = lax.all_to_all(twist_im, "tm", split_axis=2, concat_axis=1, tiled=True)
    x_re = contract("nbr,bk->nrk", part_re, cos_second) + contract(
        "nbr,bk->nrk", part_im, sin_second
    )
    x_im = contract("nbr,bk->nrk", part_im, cos_second) - contract(
        "nbr,bk->nrk", part_re, sin_second
    )
    power_bins = (x_re * x_re + x_im * x_im) / NT
    bin_total = NT // 2
    row_mean = lax.psum(jnp.sum(power_bins, axis=(1, 2)), "tm") / bin_total
    centered = power_bins - row_mean[:, None, None]
    spread = lax.psum(jnp.sum(centered * centered, axis=(1, 2)), "tm") / bin_total
    scores = centered / jnp.sqrt(spread + EPSILON)[:, None, None]
    score_flat = scores.reshape(dm_rows, per_shard * kept_bins)
    cycles = NT // (2 * HARM) // N1
    residue_tab, position_tab, base_tab, valid_tab = harmonic_tables(N1, shards, per_shard, HARM)
    my_positions = jnp.asarray(position_tab)[my_index]
    my_bases = jnp.asarray(base_tab)[my_index]
    my_valid = jnp.asarray(valid_tab)[my_index]
    cycle_ids = jnp.arange(cycles, dtype=jnp.int32)
    picked_parts = []
    for harmonic in range(1, HARM + 1):
        flat_index = (
            my_positions[harmonic - 1][:, None] * kept_bins
            + my_bases[harmonic - 1][:, None]
            + harmonic * cycle_ids[None, :]
        )
        values = jnp.take(score_flat, flat_index.reshape(-1), axis=1).reshape(dm_rows, -1, cycles)
        picked_parts.append(values * my_valid[harmonic - 1][None, :, None])
    picked = jnp.stack(picked_parts, axis=1)
    my_residues = jnp.asarray(residue_tab)[my_index].reshape(-1)
    spread_values = jnp.swapaxes(picked.reshape(dm_rows, -1, cycles), 1, 2)
    dense = jnp.zeros((dm_rows, cycles, N1), jnp.float32).at[:, :, my_residues].add(spread_values)
    dense = dense.reshape(dm_rows, cycles * N1)
    summed = lax.psum_scatter(dense.T, "tm", scatter_dimension=0, tiled=True)
    harmonic_sum = summed.T
    slot_total = cand_start.shape[3]
    offsets = jnp.arange(BW, dtype=jnp.int32)
    starts = cand_start[0, 0]
    counts = cand_count[0, 0]
    live_slots = jnp.arange(slot_total, dtype=jnp.int32)[None, :] < counts[:, None]
    markers = jnp.where(live_slots, starts, -1).astype(jnp.float32)
    bin_spans = starts[..., None] + offsets
    band_level = jnp.sum(harmonic_sum, axis=0) / dm_rows
    gathered = jnp.take(harmonic_sum, bin_spans, axis=1)
    blocks = jnp.moveaxis(gathered, 0, 2)
    blocks_in = lax.all_to_all(blocks, "dm", split_axis=0, concat_axis=0, tiled=True)
    markers_in = lax.all_to_all(markers, "dm", split_axis=0, concat_axis=0, tiled=True)
    chosen = markers_in.astype(jnp.int32)
    level = jnp.take(band_level, jnp.maximum(chosen, 0)[..., None] + offsets, axis=0)
    sifted = jnp.where(chosen[..., None] >= 0, jnp.max(blocks_in, axis=2) - level, 0.0)
    return (harmonic_sum, sifted[None, None])


def solution(mesh):
    return jax.shard_map(
        per_device,
        mesh=mesh,
        in_specs=(
            P(("beam", "dm"), "tm"),
            P(("beam", "tm"), "dm", None, None),
            P(("beam", "tm"), "dm", None),
        ),
        out_specs=(P(("beam", "dm"), "tm"), P(("beam", "tm"), "dm", None, None, None)),
        check_vma=False,
    )
```

profile of v0, /device:TPU:0, one launch (start us, length us, event | category | flops | bytes accessed | tf_op | source)
XLA Modules:
  0.0 810.9 jit_solution(11263842441877229984)
XLA Ops:
  21.3 7.4 all-to-all-done
  29.1 5.7 fusion.14
  34.9 6.1 multiply_subtract_fusion
  48.7 12.0 %all-to-all-done.1 = f32[2,256,512]{1,0,2:T(2,128)S(1)} async-done(((f32[2,256,512]{1,0,2:T(2,128)}), f32[2,256,512]{1,0,2:T(2,128)S(1)}, u32[]{:S(2)}, u32[]{:S(2)}) %all-to-all-start.1) | async-done | bytes 1048608 | tf_op jit(solution)/shard_map/all_to_all | solution.py:82
  66.1 10.5 %fusion.3 = f32[2,128,512]{2,1,0:T(8,128)} fusion(f32[2,1024,128]{1,2,0:T(8,128)S(1)} %all_to_all.53), kind=kOutput, calls=%fused_computation.17 | convolution fusion | flops 1617952768 | bytes 1572864 | tf_op jit(solution)/shard_map/nbr,bk->nrk/dot_general | solution.py:19
  85.9 10.1 %fusion.5 = f32[2,128,512]{2,1,0:T(8,128)S(1)} fusion(f32[2,1024,128]{1,2,0:T(8,128)S(1)} %all_to_all.57), kind=kOutput, calls=%fused_computation.19 | convolution fusion | flops 1617952768 | bytes 1572864 | tf_op jit(solution)/shard_map/nbr,bk->nrk/dot_general | solution.py:19
  96.0 10.0 %fusion.27 = f32[2,128,512]{2,1,0:T(8,128)S(1)} fusion(f32[2,128,512]{2,1,0:T(8,128)S(1)} %copy-done.9, f32[2,1024,128]{1,2,0:T(8,128)S(1)} %all_to_all.57), kind=kOutput, calls=%fused_computation.46 | convolution fusion | flops 1618214912 | bytes 2097152 | tf_op jit(solution)/shard_map/nbr,bk->nrk/dot_general | solution.py:19
  106.0 10.5 %fusion.99 = (f32[2]{0:T(128)S(1)}, f32[2,128,512]{2,1,0:T(8,128)S(1)}) fusion(f32[2,128,512]{2,1,0:T(8,128)S(1)} %fusion.27, f32[2,128,512]{2,1,0:T(8,128)S(1)} %fusion.5, f32[2,1024,128]{1,2,0:T(8,128)S(1)} %copy-done.1), kind=kOutput, calls=%fused_computation.178 | convolution fusion | flops 1618608128 | bytes 2621448 | tf_op jit(solution)/shard_map/nbr,bk->nrk/dot_general | solution.py:19
  116.5 5.7 psum.14
  122.5 5.7 psum.15
  128.3 16.4 %copy.140 = f32[2,128,512]{0,2,1:T(8,128)} copy(f32[2,128,512]{2,1,0:T(8,128)S(1)} %subtract_divide_fusion) | data formatting | bytes 1048576 | tf_op jit(solution)/shard_map/reshape | solution.py:96
  144.7 38.3 %gather_fusion.3 = f32[8192,2]{1,0:T(8,128)} fusion(f32[2,65536]{0,1:T(8,128)} %bitcast.136, s32[8192]{0:T(1024)S(1)} %fusion.67), kind=kCustom, calls=%fused_computation.1.clone | custom fusion | bytes 163840 | tf_op jit(solution)/shard_map/jit(_take)/gather | solution.py:110
  183.0 7.5 broadcast_select_fusion.6
  194.3 38.3 %gather_fusion.4 = f32[8192,2]{1,0:T(8,128)} fusion(f32[2,65536]{0,1:T(8,128)} %bitcast.137, s32[8192]{0:T(1024)S(1)} %fusion.68), kind=kCustom, calls=%fused_computation.2.clone | custom fusion | bytes 163840 | tf_op jit(solution)/shard_map/jit(_take)/gather | solution.py:110
  232.6 7.5 broadcast_select_fusion.5
  243.9 38.3 %gather_fusion.5 = f32[8192,2]{1,0:T(8,128)} fusion(f32[2,65536]{0,1:T(8,128)} %bitcast.138, s32[8192]{0:T(1024)S(1)} %fusion.69), kind=kCustom, calls=%fused_computation.3.clone | custom fusion | bytes 163840 | tf_op jit(solution)/shard_map/jit(_take)/gather | solution.py:110
  282.2 7.5 broadcast_select_fusion.4
  293.5 38.3 %gather_fusion.6 = f32[8192,2]{1,0:T(8,128)} fusion(f32[2,65536]{0,1:T(8,128)} %bitcast.139, s32[8192]{0:T(1024)S(1)} %fusion.70), kind=kCustom, calls=%fused_computation.4.clone | custom fusion | bytes 163840 | tf_op jit(solution)/shard_map/jit(_take)/gather | solution.py:110
  331.8 7.5 broadcast_select_fusion.3
  343.1 38.3 %gather_fusion.7 = f32[8192,2]{1,0:T(8,128)} fusion(f32[2,65536]{0,1:T(8,128)} %bitcast.140, s32[8192]{0:T(1024)S(1)} %fusion.71), kind=kCustom, calls=%fused_computation.5.clone | custom fusion | bytes 163840 | tf_op jit(solution)/shard_map/jit(_take)/gather | solution.py:110
  381.4 7.5 broadcast_select_fusion.2
  392.7 38.3 %gather_fusion.8 = f32[8192,2]{1,0:T(8,128)} fusion(f32[2,65536]{0,1:T(8,128)} %bitcast.141, s32[8192]{0:T(1024)S(1)} %fusion.72), kind=kCustom, calls=%fused_computation.6.clone | custom fusion | bytes 163840 | tf_op jit(solution)/shard_map/jit(_take)/gather | solution.py:110
  431.0 7.7 broadcast_select_fusion.1
  442.5 38.3 %gather_fusion.9 = f32[8192,2]{1,0:T(8,128)} fusion(f32[2,65536]{0,1:T(8,128)} %bitcast.142, s32[8192]{0:T(1024)S(1)} %fusion.73), kind=kCustom, calls=%fused_computation.7.clone | custom fusion | bytes 163840 | tf_op jit(solution)/shard_map/jit(_take)/gather | solution.py:110
  480.8 7.5 broadcast_select_fusion
  492.1 38.3 %gather_fusion.2 = f32[8192,2]{1,0:T(8,128)} fusion(f32[2,65536]{0,1:T(8,128)} %bitcast.143, s32[8192]{0:T(1024)S(1)} %fusion.66), kind=kCustom, calls=%fused_computation.clone | custom fusion | bytes 163840 | tf_op jit(solution)/shard_map/jit(_take)/gather | solution.py:110
  530.4 7.5 broadcast_select_fusion.7
  543.3 32.8 %scatter_fusion = f32[2,64,512]{1,0,2:T(2,128)S(1)} fusion(f32[2,64,512]{1,0,2:T(2,128)S(1)} %broadcast_in_dim.34, s32[1024]{0:T(1024)S(1)} %bitcast.172, f32[1024,2,64]{2,1,0:T(2,128)S(1)} %copy.133), kind=kCustom, calls=%fused_computation.10 | custom fusion | flops 131072 | bytes 1576960 | tf_op jit(solution)/shard_map/scatter-add | solution.py:115
  576.1 9.8 %copy.139 = f32[2,64,512]{0,2,1:T(8,128)} copy(f32[2,64,512]{1,0,2:T(2,128)S(1)} %scatter_fusion) | data formatting | bytes 524288 | tf_op jit(solution)/shard_map/reshape | solution.py:116
  586.1 126.4 %reduce-scatter.2.cloned.1.call-done = f32[8192,2]{1,0:T(8,128)} async-done(((f32[32768,2]{1,0:T(8,128)}), f32[8192,2]{1,0:T(8,128)}) %reduce-scatter.2.cloned.1.call-update) | async-done | bytes 65552 | tf_op jit(solution)/shard_map/reduce_scatter | solution.py:117
  712.5 30.0 %gather_fusion = f32[8192,2]{1,0:T(8,128)} fusion(f32[2,8192]{0,1:T(8,128)} %bitcast.144, s32[8192]{0:T(1024)S(1)} %broadcast_clamp_fusion.1), kind=kCustom, calls=%fused_computation.8 | custom fusion | bytes 163840 | tf_op jit(solution)/shard_map/jit(_take)/gather | solution.py:127
  757.5 45.5 %gather_fusion.1 = f32[8192]{0:T(1024)S(1)} fusion(f32[8192]{0:T(1024)S(1)} %broadcast_multiply_fusion, s32[8192]{0:T(1024)S(1)} %broadcast_clamp_fusion), kind=kCustom, calls=%fused_computation.9 | custom fusion | bytes 98304 | tf_op jit(solution)/shard_map/jit(_take)/gather | solution.py:132
  (117 shorter events, 84.4 us)
Async XLA Ops:
  8.7 6.9 copy-start.5
  10.0 18.7 %all-to-all-start = ((f32[2,128,1024]{1,0,2:T(2,128)}), f32[2,128,1024]{1,0,2:T(2,128)S(1)}, u32[]{:S(2)}, u32[]{:S(2)}) async-start(f32[2,128,1024]{1,0,2:T(2,128)} %copy.110), calls=%async_computation | async-start | bytes 2097152 | tf_op jit(solution)/shard_map/all_to_all | solution.py:75
  42.7 17.9 %all-to-all-start.1 = ((f32[2,256,512]{1,0,2:T(2,128)}), f32[2,256,512]{1,0,2:T(2,128)S(1)}, u32[]{:S(2)}, u32[]{:S(2)}) async-start(f32[2,256,512]{1,0,2:T(2,128)} %copy.113), calls=%async_computation.1 | async-start | bytes 2097152 | tf_op jit(solution)/shard_map/all_to_all | solution.py:82
  46.9 17.3 %copy-start.6 = (s32[1,1,4,16]{3,2,1,0:T(4,128)S(1)}, s32[1,1,4,16]{3,2,1,0:T(4,128)}, u32[]{:S(2)}) copy-start(s32[1,1,4,16]{3,2,1,0:T(4,128)} %param.10) | copy-start | bytes 772
  46.9 17.3 %copy-start.8 = (s32[1,1,4]{2,1,0:T(1,128)S(1)}, s32[1,1,4]{2,1,0:T(1,128)}, u32[]{:S(2)}) copy-start(s32[1,1,4]{2,1,0:T(1,128)} %param.11) | copy-start | bytes 52
  60.7 17.9 %all-to-all-start.2 = ((f32[2,256,512]{1,0,2:T(2,128)}), f32[2,256,512]{1,0,2:T(2,128)S(1)}, u32[]{:S(2)}, u32[]{:S(2)}) async-start(f32[2,256,512]{1,0,2:T(2,128)} %copy.115), calls=%async_computation.2 | async-start | bytes 2097152 | tf_op jit(solution)/shard_map/all_to_all | solution.py:83
  66.1 10.5 %copy-start = (f32[2,1024,128]{1,2,0:T(8,128)}, f32[2,1024,128]{1,2,0:T(8,128)S(1)}, u32[]{:S(2)}) copy-start(f32[2,1024,128]{1,2,0:T(8,128)S(1)} %all_to_all.53) | copy-start | bytes 3145732
  78.6 43.9 %all-to-all-start.3 = ((f32[4,1,16]{2,1,0:T(1,128)}), f32[4,1,16]{2,1,0:T(1,128)S(1)}, u32[]{:S(2)}, u32[]{:S(2)}) async-start(f32[4,1,16]{2,1,0:T(1,128)} %bitcast.45), calls=%async_computation.4 | async-start | bytes 4096 | tf_op jit(solution)/shard_map/all_to_all | solution.py:130
  84.2 628.3 %reduce-scatter.2.cloned.1.call-start = ((), (), s32[]{:S(2)}) async-start(), calls=%async_computation.6 | async-start | bytes 20971520 | tf_op jit(solution)/shard_map/reduce_scatter | solution.py:117
  85.9 10.1 %copy-start.9 = (f32[2,128,512]{2,1,0:T(8,128)S(1)}, f32[2,128,512]{2,1,0:T(8,128)}, u32[]{:S(2)}) copy-start(f32[2,128,512]{2,1,0:T(8,128)} %fusion.3) | copy-start | bytes 1572868
  96.0 10.0 %copy-start.1 = (f32[2,1024,128]{1,2,0:T(8,128)S(1)}, f32[2,1024,128]{1,2,0:T(8,128)}, u32[]{:S(2)}) copy-start(f32[2,1024,128]{1,2,0:T(8,128)} %copy-done) | copy-start | bytes 3145732
  289.7 42.1 %copy-start.3 = (pred[8192]{0:T(1024)(128)(4,1)S(1)}, pred[8192]{0:T(1024)(128)(4,1)}, u32[]{:S(2)}) copy-start(pred[8192]{0:T(1024)(128)(4,1)} %compare_and_fusion.3) | copy-start | bytes 24580
  339.3 42.1 %copy-start.2 = (pred[8192]{0:T(1024)(128)(4,1)S(1)}, pred[8192]{0:T(1024)(128)(4,1)}, u32[]{:S(2)}) copy-start(pred[8192]{0:T(1024)(128)(4,1)} %compare_and_fusion.2) | copy-start | bytes 24580
  541.7 1.7 copy-start.7
  742.5 2.9 copy-start.4
  746.0 57.0 %all-to-all-start.4 = ((f32[4,16,2,128]{3,1,2,0:T(8,128)}), f32[4,16,2,128]{3,1,2,0:T(8,128)S(1)}, u32[]{:S(2)}, u32[]{:S(2)}) async-start(f32[4,16,2,128]{3,1,2,0:T(8,128)} %select_bitcast_fusion), calls=%async_computation.5 | async-start | bytes 131072 | tf_op jit(solution)/shard_map/all_to_all | solution.py:129
Sparse Core Ops, SparseCore 0:
  586.1 126.3 reduce-scatter.1
where the time goes:
time: 822 us; the launch traced here: 811 us
  local copies, waits for them, and re-layouts  458 us (56%)
  waiting for transfers between devices  148 us (18%)
  other arithmetic  104 us (13%)
  matrix products  52.8 us (6%)
  starting transfers between devices  21.9 us (3%)
  between operations  14.9 us (2%)
  blocking collectives  11.4 us (1%)
    gather x8, local copies, waits for them, and re-layouts, per_device(): jnp.take(score_flat, flat_index.reshape(-1), axis=1)  307 us
    reduce_scatter x1, waiting for transfers between devices, per_device(): summed = lax.psum_scatter(dense.T, 'tm', scatter_dimension=0, tiled=True)  126 us
    select_n x8, other arithmetic, per_device(): jnp.take(score_flat, flat_index.reshape(-1), axis=1)  60.3 us
    dot_general x6, matrix products, contract(): return jnp.einsum(pattern, left, right, precision=lax.Precision.HIGHEST)  52.8 us
    gather x1, local copies, waits for them, and re-layouts, per_device(): jnp.take(band_level, jnp.maximum(chosen, 0)[..., None] + offsets, axis=0)  45.5 us
    gather x2, local copies, waits for them, and re-layouts, per_device(): gathered = jnp.take(harmonic_sum, bin_spans, axis=1)  32.9 us
    scatter-add x1, other arithmetic, per_device(): jnp.zeros((dm_rows, cycles, N1), jnp.float32).at[:, :, my_residues]  32.8 us
    reshape x8, local copies, waits for them, and re-layouts, per_device(): jnp.take(score_flat, flat_index.reshape(-1), axis=1)  29.9 us
  transfers between devices with their start and end apart: 6, of which 4 were waited for; matrix products, arithmetic and copies ran while one was open for 13% of the time, Pallas kernels for 0%

commit v1 on v0

--- a/solution.py
+++ b/solution.py
@@ -4,6 +4,8 @@
 import jax.numpy as jnp
 import numpy as np
 from jax import lax
+from jax.experimental import pallas as pl
+from jax.experimental.pallas import tpu as pltpu
 from jax.sharding import PartitionSpec as P
 
 NT = 524288
@@ -134,9 +136,371 @@
     return (harmonic_sum, sifted[None, None])
 
 
+MESH = pl.DeviceIdType.MESH
+LANES = 128
+CHUNKS = 4
+VMEM_LIMIT = 60 * 1024 * 1024
+
+
+def split_pair(value):
+    high = value.astype(jnp.bfloat16)
+    return high, (value - high.astype(jnp.float32)).astype(jnp.bfloat16)
+
+
+def host_split(table):
+    high = table.astype(jnp.bfloat16)
+    low = (table - high.astype(np.float64)).astype(jnp.bfloat16)
+    return high, low
+
+
+def dft_tables(shards, cores):
+    inner = NT // N1
+    kept = inner // 2
+    coarse = N1 // shards
+    res = N1 // cores
+    ids = np.arange(N1)
+    turn = 2.0 * np.pi * (np.outer(ids, ids) % N1) / N1
+    first = np.empty((cores, shards, 2 * res, 3 * coarse), jnp.bfloat16)
+    for core in range(cores):
+        for shard in range(shards):
+            part = turn[core * res : (core + 1) * res, shard * coarse : (shard + 1) * coarse]
+            high, low = host_split(np.concatenate([np.cos(part), -np.sin(part)], axis=0))
+            first[core, shard] = np.concatenate([high, high, low], axis=1)
+    turn = 2.0 * np.pi * np.outer(ids, np.arange(inner)) / NT
+    twist_tab = np.stack([np.cos(turn), np.sin(turn)], axis=0).astype(np.float32)
+    twist_tab = twist_tab.reshape(2, cores, res, inner).transpose(1, 0, 2, 3)
+    turn = 2.0 * np.pi * (np.outer(np.arange(kept), np.arange(inner)) % inner) / inner
+    second = np.stack(host_split(np.cos(turn)) + host_split(np.sin(turn)), axis=0)
+    return first, twist_tab, second
+
+
+def spectrum_kernel(
+    x_ref, first_hbm, twist_hbm, second_hbm, out_ref,
+    gathered, outgoing, x_tab, first, twist_tab, second, partial, b_high, b_low, power, picks, select,
+    load_sem, send_sem, recv_sem,
+):
+    me = lax.axis_index("tm")
+    core, chip = lax.rem(me, 2), me // 2
+    sibling = me + 1 - 2 * core
+    across = lax.rem(me + 2, 4)
+    diagonal = lax.rem(sibling + 2, 4)
+    size = gathered.shape[1]
+    step = size // CHUNKS
+    shards, inner = gathered.shape[0], partial.shape[1]
+    coarse = size // (inner // LANES)
+    res = partial.shape[0] // 2
+    kept = power.shape[1]
+
+    loads = [
+        pltpu.make_async_copy(first_hbm.at[core], first, load_sem.at[0]),
+        pltpu.make_async_copy(twist_hbm.at[core], twist_tab, load_sem.at[1]),
+        pltpu.make_async_copy(second_hbm, second, load_sem.at[2]),
+    ]
+    for load in loads:
+        load.start()
+    barrier = pltpu.get_barrier_semaphore()
+    for peer in (sibling, across):
+        pl.semaphore_signal(barrier, inc=1, device_id={"tm": peer}, device_id_type=MESH)
+    for piece in range(CHUNKS):
+        row_a = x_ref[pl.ds(2 * piece * step, step, stride=2), :]
+        row_b = x_ref[pl.ds(2 * piece * step + 1, step, stride=2), :]
+        outgoing[piece * step : (piece + 1) * step, :] = jnp.where(chip == 0, row_b, row_a)
+        gathered[me, piece * step : (piece + 1) * step, :] = jnp.where(chip == 0, row_a, row_b)
+    pl.semaphore_wait(barrier, 2)
+
+    def remote(src, dst, index, peer):
+        return pltpu.make_async_remote_copy(
+            src_ref=src, dst_ref=dst, send_sem=send_sem.at[index], recv_sem=recv_sem.at[index],
+            device_id={"tm": peer}, device_id_type=MESH,
+        )
+
+    crossing = []
+    for piece in range(CHUNKS):
+        rows = pl.ds(piece * step, step)
+        crossing.append(remote(outgoing.at[rows], gathered.at[me, rows], 1 + piece, across))
+        crossing[-1].start()
+    own = remote(gathered.at[me], gathered.at[me], 0, sibling)
+    own.start()
+
+    lane_ids = lax.broadcasted_iota(jnp.int32, (res, N1), 1)
+    res_ids = lax.broadcasted_iota(jnp.int32, (res, N1), 0) + core * res
+    slot = 0
+    for harmonic in range(1, HARM + 1):
+        target = lane_ids * harmonic - res_ids
+        for cycle in range(harmonic):
+            hit = jnp.where(target == cycle * N1, 1.0, 0.0)
+            select[slot * res : (slot + 1) * res, :] = hit.astype(jnp.bfloat16)
+            slot += 1
+    for load in loads:
+        load.wait()
+
+    def accumulate(shard, fresh):
+        for group in range(inner // LANES):
+            high, low = split_pair(gathered[shard, pl.ds(group, coarse, stride=inner // LANES), :])
+            cols = slice(group * LANES, (group + 1) * LANES)
+            x_tab[0:coarse, cols] = high
+            x_tab[coarse : 2 * coarse, cols] = low
+            x_tab[2 * coarse : 3 * coarse, cols] = high
+        for block in range(inner // 256):
+            cols = slice(block * 256, (block + 1) * 256)
+            term = jnp.dot(first[shard], x_tab[:, cols], preferred_element_type=jnp.float32)
+            partial[:, cols] = term if fresh else partial[:, cols] + term
+
+    accumulate(me, True)
+    own.wait_recv()
+    accumulate(sibling, False)
+    forwards = []
+    for piece in range(CHUNKS):
+        rows = pl.ds(piece * step, step)
+        crossing[piece].wait_recv()
+        forwards.append(remote(gathered.at[across, rows], gathered.at[across, rows], 1 + CHUNKS + piece, sibling))
+        forwards[-1].start()
+    accumulate(across, False)
+    for forward in forwards:
+        forward.wait_recv()
+    accumulate(diagonal, False)
+
+    for block in range(inner // 256):
+        cols = slice(block * 256, (block + 1) * 256)
+        real_part, imag_part = twist(
+            partial[0:res, cols], partial[res : 2 * res, cols], twist_tab[0, :, cols], twist_tab[1, :, cols]
+        )
+        b_high[0:res, cols], b_low[0:res, cols] = split_pair(real_part)
+        b_high[res : 2 * res, cols], b_low[res : 2 * res, cols] = split_pair(imag_part)
+
+    def against(table, right):
+        return lax.dot_general(table, right, (((1,), (1,)), ((), ())), preferred_element_type=jnp.float32)
+
+    half = kept // 2
+
+    @pl.loop(0, 2)
+    def _(part):
+        rows = pl.ds(pl.multiple_of(part * half, half), half)
+        by_cos = against(second[0, rows], b_high[...]) + against(second[0, rows], b_low[...])
+        by_cos = by_cos + against(second[1, rows], b_high[...])
+        by_sin = against(second[2, rows], b_high[...]) + against(second[2, rows], b_low[...])
+        by_sin = by_sin + against(second[3, rows], b_high[...])
+        x_re = by_cos[:, 0:res] + by_sin[:, res:]
+        x_im = by_cos[:, res:] - by_sin[:, 0:res]
+        bins = (x_re * x_re + x_im * x_im) / NT
+        for column in range(res // LANES):
+            power[column, rows, :] = bins[:, column * LANES : (column + 1) * LANES]
+
+    total = jnp.sum(power[...])
+    mean = total / (kept * res)
+    off = power[...] - mean
+    deviation = jnp.sum(off * off)
+
+    cycles = NT // (2 * HARM) // N1
+    slot = 0
+    for harmonic in range(1, HARM + 1):
+        for cycle in range(harmonic):
+            for column in range(res // LANES):
+                high, low = split_pair(power[column, pl.ds(cycle, cycles, stride=harmonic), :])
+                cols = slice(slot * res + column * LANES, slot * res + (column + 1) * LANES)
+                picks[0:cycles, cols] = high
+                picks[cycles : 2 * cycles, cols] = low
+            slot += 1
+    sums = jnp.dot(picks[...], select[...], preferred_element_type=jnp.float32)
+    sums = sums[0:cycles] + sums[cycles : 2 * cycles]
+    each = cycles // shards
+    lead = N1 // LANES
+    for shard in range(shards):
+        for column in range(lead):
+            out_ref[shard, column * each : (column + 1) * each, :] = sums[
+                shard * each : (shard + 1) * each, column * LANES : (column + 1) * LANES
+            ]
+        out_ref[shard, lead * each : lead * each + 8, :] = jnp.full((8, LANES), mean, jnp.float32)
+        out_ref[shard, lead * each + 8 : lead * each + 16, :] = jnp.full((8, LANES), deviation, jnp.float32)
+    own.wait_send()
+    for copy in crossing + forwards:
+        copy.wait_send()
+
+
+def exchange_kernel(
+    part_ref, mark_ref, harm_ref, level_ref, peaks_ref, marks_ref,
+    parts, marks, peaks, top, send_sem, recv_sem,
+):
+    me, band = lax.axis_index("tm"), lax.axis_index("dm")
+    shards, bands = lax.axis_size("tm"), lax.axis_size("dm")
+    lead = N1 // LANES
+    each = (part_ref.shape[1] - 16) // lead
+
+    barrier = pltpu.get_barrier_semaphore()
+    for axis, count, here in (("tm", shards, me), ("dm", bands, band)):
+        for away in range(1, count):
+            peer = lax.rem(here + away, count)
+            pl.semaphore_signal(barrier, inc=1, device_id={axis: peer}, device_id_type=MESH)
+    pl.semaphore_wait(barrier, shards + bands - 2)
+
+    def remote(src, dst, index, axis, peer):
+        return pltpu.make_async_remote_copy(
+            src_ref=src, dst_ref=dst, send_sem=send_sem.at[index], recv_sem=recv_sem.at[index],
+            device_id={axis: peer}, device_id_type=MESH,
+        )
+
+    first_hop, second_hop, third_hop = [], [], []
+    for away in range(1, shards):
+        peer = lax.rem(me + away, shards)
+        first_hop.append(remote(part_ref.at[peer], parts.at[me], away - 1, "tm", peer))
+        first_hop[-1].start()
+    for away in range(1, bands):
+        peer = lax.rem(band + away, bands)
+        second_hop.append(remote(mark_ref.at[peer], marks.at[band], shards + away, "dm", peer))
+        second_hop[-1].start()
+    for copy in first_hop:
+        copy.wait_recv()
+    parts[me] = part_ref[me]
+
+    bin_total = NT // 2
+    share = bin_total // 2
+    rows = []
+    for row in range(2):
+        left, right = parts[2 * row], parts[2 * row + 1]
+        base = lead * each
+        mean_l, mean_r = left[base : base + 8], right[base : base + 8]
+        row_mean = 0.5 * (mean_l + mean_r)
+        gap_l, gap_r = mean_l - row_mean, mean_r - row_mean
+        deviation = left[base + 8 : base + 16] + right[base + 8 : base + 16]
+        spread = (deviation + share * (gap_l * gap_l + gap_r * gap_r)) / bin_total
+        scale = jnp.sqrt(spread + EPSILON)
+        rows.append((left[:base] + right[:base] - HARM * row_mean[0:1]) / scale[0:1])
+    highest = jnp.maximum(rows[0], rows[1])
+    level = (rows[0] + rows[1]) / 2
+    for column in range(lead):
+        block = slice(column * each, (column + 1) * each)
+        top[pl.ds(column, each, stride=lead), :] = highest[block]
+        level_ref[pl.ds(column, each, stride=lead), :] = level[block]
+        for row in range(2):
+            harm_ref[pl.ds(2 * column + row, each, stride=2 * lead), :] = rows[row][block]
+    for away in range(1, bands):
+        peer = lax.rem(band + away, bands)
+        third_hop.append(remote(top, peaks.at[band], shards + bands + away, "dm", peer))
+        third_hop[-1].start()
+    for copy in second_hop + third_hop:
+        copy.wait_recv()
+    peaks[band] = top[...]
+    marks[band] = mark_ref[band]
+    peaks_ref[...] = peaks[...]
+    marks_ref[...] = marks[...]
+    for copy in first_hop + second_hop + third_hop:
+        copy.wait_send()
+
+
+def sift_kernel(level_ref, peaks_ref, marks_ref, out_ref):
+    bands, slots, width = out_ref.shape
+    blocks = level_ref.shape[0]
+    ids = lax.broadcasted_iota(jnp.int32, (slots, blocks), 1)
+    lanes = lax.broadcasted_iota(jnp.int32, (slots, width), 1)
+    for source in range(bands):
+        start = marks_ref[source]
+        safe = jnp.maximum(start, 0)
+        block, offset = safe // LANES, safe % LANES
+        excess = peaks_ref[source] - level_ref[...]
+
+        def pick(which):
+            hot = jnp.where(ids == which[:, 0:1], 1.0, 0.0)
+            return jnp.dot(hot, excess, precision=lax.Precision.HIGHEST, preferred_element_type=jnp.float32)
+
+        lower, upper = pick(block), pick(block + 1)
+        place = lanes + offset
+        index = place % LANES
+        joined = jnp.where(
+            place < LANES, jnp.take_along_axis(lower, index, axis=1), jnp.take_along_axis(upper, index, axis=1)
+        )
+        out_ref[source] = jnp.where(start >= 0, joined, 0.0)
+
+
+def fast_device(tables, series, cand_start, cand_count):
+    first, twist_tab, second = tables
+    dm_rows, samples_dev = series.shape
+    shards, bands = lax.axis_size("tm"), lax.axis_size("dm")
+    inner, cores = NT // N1, 2
+    res, coarse, kept = N1 // cores, N1 // shards, inner // 2
+    size = samples_dev // LANES
+    cycles = NT // (2 * HARM) // N1
+    each, lead = cycles // shards, N1 // LANES
+    steps = HARM * (HARM + 1) // 2
+    slots = cand_start.shape[3]
+    vmem, anywhere = pl.BlockSpec(memory_space=pltpu.VMEM), pl.BlockSpec(memory_space=pl.ANY)
+    lined = series.reshape(dm_rows, size, LANES).swapaxes(0, 1).reshape(size * dm_rows, LANES)
+    width = lead * each + 16
+    moved = pl.pallas_call(
+        spectrum_kernel,
+        out_shape=jax.ShapeDtypeStruct((shards, width, LANES), jnp.float32),
+        in_specs=[vmem, anywhere, anywhere, anywhere],
+        out_specs=vmem,
+        scratch_shapes=[
+            pltpu.VMEM((shards, size, LANES), jnp.float32),
+            pltpu.VMEM((size, LANES), jnp.float32),
+            pltpu.VMEM((3 * coarse, inner), jnp.bfloat16),
+            pltpu.VMEM(first.shape[1:], jnp.bfloat16),
+            pltpu.VMEM(twist_tab.shape[1:], jnp.float32),
+            pltpu.VMEM(second.shape, jnp.bfloat16),
+            pltpu.VMEM((2 * res, inner), jnp.float32),
+            pltpu.VMEM((2 * res, inner), jnp.bfloat16),
+            pltpu.VMEM((2 * res, inner), jnp.bfloat16),
+            pltpu.VMEM((res // LANES, kept, LANES), jnp.float32),
+            pltpu.VMEM((2 * cycles, steps * res), jnp.bfloat16),
+            pltpu.VMEM((steps * res, N1), jnp.bfloat16),
+            pltpu.SemaphoreType.DMA((3,)),
+            pltpu.SemaphoreType.DMA((1 + 2 * CHUNKS,)),
+            pltpu.SemaphoreType.DMA((1 + 2 * CHUNKS,)),
+        ],
+        compiler_params=pltpu.CompilerParams(
+            collective_id=0, has_side_effects=True, vmem_limit_bytes=VMEM_LIMIT
+        ),
+    )(lined, jnp.asarray(first), jnp.asarray(twist_tab), jnp.asarray(second))
+    live = jnp.arange(slots, dtype=jnp.int32)[None, :] < cand_count[0, 0][:, None]
+    marks = jnp.where(live, cand_start[0, 0], -1)
+    marks = jnp.broadcast_to(marks[..., None], (bands, slots, LANES))
+    blocks = lead * each
+    harm, level, peaks, marks_in = pl.pallas_call(
+        exchange_kernel,
+        out_shape=(
+            jax.ShapeDtypeStruct((dm_rows * blocks, LANES), jnp.float32),
+            jax.ShapeDtypeStruct((blocks, LANES), jnp.float32),
+            jax.ShapeDtypeStruct((bands, blocks, LANES), jnp.float32),
+            jax.ShapeDtypeStruct((bands, slots, LANES), jnp.int32),
+        ),
+        in_specs=[vmem, vmem],
+        out_specs=(vmem,) * 4,
+        scratch_shapes=[
+            pltpu.VMEM((shards, width, LANES), jnp.float32),
+            pltpu.VMEM((bands, slots, LANES), jnp.int32),
+            pltpu.VMEM((bands, blocks, LANES), jnp.float32),
+            pltpu.VMEM((blocks, LANES), jnp.float32),
+            pltpu.SemaphoreType.DMA((shards + 2 * bands,)),
+            pltpu.SemaphoreType.DMA((shards + 2 * bands,)),
+        ],
+        compiler_params=pltpu.CompilerParams(collective_id=1, has_side_effects=True),
+    )(moved, marks)
+    sifted = pl.pallas_call(
+        sift_kernel,
+        out_shape=jax.ShapeDtypeStruct((bands, slots, BW), jnp.float32),
+        in_specs=[vmem] * 3,
+        out_specs=vmem,
+    )(level, peaks, marks_in)
+    harmonic_sum = harm.reshape(blocks, dm_rows, LANES).swapaxes(0, 1).reshape(dm_rows, blocks * LANES)
+    return (harmonic_sum, sifted[None, None])
+
+
+def fits(mesh):
+    return mesh.shape["tm"] == 4 and BW == LANES
+
+
 def solution(mesh):
+    if fits(mesh):
+        tables = dft_tables(mesh.shape["tm"], 2)
+
+        def body(series, cand_start, cand_count):
+            if series.shape[0] != 2:
+                return per_device(series, cand_start, cand_count)
+            return fast_device(tables, series, cand_start, cand_count)
+    else:
+        body = per_device
     return jax.shard_map(
-        per_device,
+        body,
         mesh=mesh,
         in_specs=(
             P(("beam", "dm"), "tm"),

time: 822 us -> 43.7 us (0.05); the launches traced: 811 us -> 43.4 us
  local copies, waits for them, and re-layouts: 458 us -> 2.16 us
  waiting for transfers between devices: 148 us -> 0 us
  other arithmetic: 104 us -> 0.75 us
  matrix products: 52.8 us -> 0 us
  Pallas kernels: 0 us -> 39.9 us
  starting transfers between devices: 21.9 us -> 0 us
  between operations: 14.9 us -> 0.65 us
  blocking collectives: 11.4 us -> 0 us
    gather x11 -> x0, local copies, waits for them, and re-layouts: 385 us -> none  [the longest x8 307 us: per_device(): jnp.take(score_flat, flat_index.reshape(-1), axis=1)]
    reduce_scatter x1 -> x0, waiting for transfers between devices: 126 us -> none  [per_device(): summed = lax.psum_scatter(dense.T, 'tm', scatter_dimension=0, tiled=True)]
    select_n x13 -> x1, other arithmetic: 62.3 us -> 0.75 us  [fast_device(): marks = jnp.where(live, cand_start[0, 0], -1)]
    reshape x12 -> x0, local copies, waits for them, and re-layouts: 57.6 us -> none  [the longest x8 29.9 us: per_device(): jnp.take(score_flat, flat_index.reshape(-1), axis=1)]
    dot_general x6 -> x0, matrix products: 52.8 us -> none  [contract(): return jnp.einsum(pattern, left, right, precision=lax.Precision.HIGHEST)]
    pallas_call x0 -> x3, Pallas kernels: none -> 39.9 us  [the longest x1 24.6 us: fast_device(): pl.pallas_call(spectrum_kernel, out_shape=jax.ShapeDtypeStruct((shards, w...]
    scatter-add x1 -> x0, other arithmetic: 32.8 us -> none  [per_device(): jnp.zeros((dm_rows, cycles, N1), jnp.float32).at[:, :, my_residues]]
    all_to_all x5 -> x0, starting transfers between devices: 21.5 us -> none  [the longest x1 5.6 us: per_device(): lax.all_to_all(markers, 'dm', split_axis=0, concat_axis=0, tiled=True)]
  transfers between devices with their start and end apart: 6 -> 0, of which waited for: 4 -> 0; matrix products, arithmetic and copies ran while one was open for 13% -> 0% of each run, Pallas kernels for 0% -> 0%
where the time goes in v1:
time: 43.7 us; the launch traced here: 43.4 us
  Pallas kernels  39.9 us (91%)
  local copies, waits for them, and re-layouts  2.16 us (5%)
  other arithmetic  0.75 us (2%)
  between operations  0.65 us (1%)
    pallas_call x1, Pallas kernels, fast_device(): pl.pallas_call(spectrum_kernel, out_shape=jax.ShapeDtypeStruct((shards, w...  24.6 us
    pallas_call x1, Pallas kernels, fast_device(): pl.pallas_call(exchange_kernel, out_shape=(jax.ShapeDtypeStruct((dm_rows...  13.3 us
    pallas_call x1, Pallas kernels, fast_device(): pl.pallas_call(sift_kernel, out_shape=jax.ShapeDtypeStruct((bands, slots,...  1.98 us
    unnamed x1, local copies, waits for them, and re-layouts  1.47 us

profile of v1, /device:TPU:0, one launch (start us, length us, event | category | flops | bytes accessed | tf_op | source)
XLA Modules:
  0.0 43.4 jit_solution(16697190621491246150)
XLA Ops:
  0.6 0.8 %bitcast_select_fusion = s32[4,16]{1,0:T(4,128)S(1)} fusion(s32[1,1,4,16]{3,2,1,0:T(4,128)} %param.7, s32[4]{0:T(128)} %bitcast.17), kind=kLoop, calls=%fused_computation | loop fusion | flops 128 | bytes 528 | tf_op jit(solution)/shard_map/jit(_where)/select_n | solution.py:455
  1.4 0.7 %broadcast_in_dim.15.mark_ref = s32[4,16,128]{2,1,0:T(8,128)} broadcast(s32[4,16]{1,0:T(4,128)S(1)} %bitcast_select_fusion), dimensions={0,1} | broadcast | bytes 33024 | tf_op jit(solution)/shard_map/broadcast_in_dim | solution.py:456
  2.1 24.6 %shard_map.77.part_ref = f32[4,80,128]{2,1,0:T(8,128)} custom-call(f32[2048,128]{1,0:T(8,128)} %bitcast.14, bf16[2,4,512,384]{3,2,1,0:T(8,128)(2,1)} %constant.8.clone.first_hbm, f32[2,2,256,1024]{3,2,1,0:T(8,128)} %constant.9.clone.twist_hbm, bf16[4,512,1024]{2,1,0:T(8,128)(2,1)} %constant.10.clone.second_hbm), custom_call_target="tpu_custom_call" | custom-call | tf_op jit(solution)/shard_map/pallas_call | solution.py:428
  26.7 13.3 %shard_map.78 = (f32[128,128]{1,0:T(8,128)}, f32[64,128]{1,0:T(8,128)}, f32[4,64,128]{2,1,0:T(8,128)}, s32[4,16,128]{2,1,0:T(8,128)}) custom-call(f32[4,80,128]{2,1,0:T(8,128)} %shard_map.77.part_ref, s32[4,16,128]{2,1,0:T(8,128)} %broadcast_in_dim.15.mark_ref), custom_call_target="tpu_custom_call" | custom-call | tf_op jit(solution)/shard_map/pallas_call | solution.py:458
  40.0 2.0 %shard_map.79 = f32[4,16,128]{2,1,0:T(8,128)} custom-call(f32[64,128]{1,0:T(8,128)} %get-tuple-element.7.level_ref, f32[4,64,128]{2,1,0:T(8,128)} %get-tuple-element.8.peaks_ref, s32[4,16,128]{2,1,0:T(8,128)} %get-tuple-element.9.marks_ref), custom_call_target="tpu_custom_call" | custom-call | tf_op jit(solution)/shard_map/pallas_call | solution.py:478
  42.0 1.5 %copy.11 = f32[2,8192]{1,0:T(2,128)} copy(f32[2,8192]{1,0:T(2,128)} %bitcast.15) | data formatting | bytes 131072

commit v2 on v0

--- a/solution.py
+++ b/solution.py
@@ -4,6 +4,8 @@
 import jax.numpy as jnp
 import numpy as np
 from jax import lax
+from jax.experimental import pallas as pl
+from jax.experimental.pallas import tpu as pltpu
 from jax.sharding import PartitionSpec as P
 
 NT = 524288
@@ -134,9 +136,423 @@
     return (harmonic_sum, sifted[None, None])
 
 
+MESH = pl.DeviceIdType.MESH
+LANES = 128
+CHUNKS = 4
+VMEM_LIMIT = 60 * 1024 * 1024
+
+
+def split_pair(value):
+    high = value.astype(jnp.bfloat16)
+    return high, (value - high.astype(jnp.float32)).astype(jnp.bfloat16)
+
+
+def host_split(table):
+    high = table.astype(jnp.bfloat16)
+    low = (table - high.astype(np.float64)).astype(jnp.bfloat16)
+    return high, low
+
+
+def dft_tables(shards):
+    inner = NT // N1
+    kept = inner // 2
+    piece = N1 // shards // CHUNKS
+    res = N1 // 2
+    ids = np.arange(res)
+    first = np.empty((shards // 2, CHUNKS, 2 * res, shards // 2, 2, piece), jnp.bfloat16)
+    for shard in range(shards):
+        for chunk in range(CHUNKS):
+            coarse = (shard * CHUNKS + chunk) * piece + np.arange(piece)
+            turn = 2.0 * np.pi * (np.outer(ids, coarse) % N1) / N1
+            pair = host_split(np.concatenate([np.cos(turn), -np.sin(turn)], axis=0))
+            for part in range(2):
+                first[shard // 2, chunk, :, shard % 2, part] = pair[part]
+    first = first.reshape(shards // 2, CHUNKS, 2 * res, 2 * shards // 2 * piece)
+
+    def waves(turn):
+        return np.stack([np.cos(turn), np.sin(turn)], axis=0).astype(np.float32)
+
+    lanes = np.arange(LANES)
+    twists = np.stack(
+        [
+            waves(2.0 * np.pi * np.outer(ids, lanes) / NT),
+            waves(2.0 * np.pi * np.outer(ids, np.full(LANES, LANES)) / NT),
+        ],
+        axis=0,
+    )
+    shift = waves(2.0 * np.pi * np.outer(np.full(8, res), lanes) / NT)
+    second = np.empty((4, kept, inner // 4), jnp.bfloat16)
+    for kind in range(4):
+        turn = np.outer(4 * np.arange(kept // 4) + kind, np.arange(inner // 4)) % inner
+        turn = 2.0 * np.pi * turn / inner
+        cos_pair, sin_pair = host_split(np.cos(turn)), host_split(np.sin(turn))
+        second[kind] = np.concatenate([cos_pair[0], sin_pair[0], cos_pair[1], sin_pair[1]], axis=0)
+    return first, twists, shift, second
+
+
+def turned(left, right):
+    return left[0] * right[0] - left[1] * right[1], left[0] * right[1] + left[1] * right[0]
+
+
+def windows(table, start):
+    count, blocks = start.shape[0], table.shape[0]
+    high = table.astype(jnp.bfloat16)
+    rest = table - high.astype(jnp.float32)
+    middle = rest.astype(jnp.bfloat16)
+    low = (rest - middle.astype(jnp.float32)).astype(jnp.bfloat16)
+    block = start // LANES
+    ids = lax.broadcasted_iota(jnp.int32, (count, blocks), 1)
+    hot = jnp.concatenate(
+        [jnp.where(ids == block[:, 0:1], 1.0, 0.0), jnp.where(ids == block[:, 0:1] + 1, 1.0, 0.0)], axis=0
+    ).astype(jnp.bfloat16)
+    picked = jnp.dot(hot, jnp.concatenate([high, middle, low], axis=1), preferred_element_type=jnp.float32)
+    picked = picked[:, 0:LANES] + picked[:, LANES : 2 * LANES] + picked[:, 2 * LANES :]
+    place = lax.broadcasted_iota(jnp.int32, (count, LANES), 1) + start % LANES
+    index = place % LANES
+    return jnp.where(
+        place < LANES,
+        jnp.take_along_axis(picked[0:count], index, axis=1),
+        jnp.take_along_axis(picked[count:], index, axis=1),
+    )
+
+
+def search_kernel(
+    x_ref, start_ref, count_ref, first_hbm, twists_ref, shift_ref, second_hbm, harm_ref, sift_ref,
+    gathered, outgoing, x_tab, first, twist_tab, second, partial, b_high, b_low, power, picks, select,
+    mine, parts, marks_out, marks, tops_out, tops, flat_top, flat_level,
+    load_sem, send_sem, recv_sem, hop_send, hop_recv,
+):
+    me, band = lax.axis_index("tm"), lax.axis_index("dm")
+    shards, bands = lax.axis_size("tm"), lax.axis_size("dm")
+    core, chip = lax.rem(me, 2), me // 2
+    sibling = me + 1 - 2 * core
+    across = lax.rem(me + 2, 4)
+    size = gathered.shape[1]
+    step = size // CHUNKS
+    inner = partial.shape[1]
+    groups = inner // LANES
+    piece_rows = step // groups
+    res = partial.shape[0] // 2
+    kept = power.shape[1]
+    slots = sift_ref.shape[1]
+
+    width = first_hbm.shape[3]
+    loads = [
+        pltpu.make_async_copy(first_hbm, first.at[:, :, :, pl.ds(0, width)], load_sem.at[0]),
+        pltpu.make_async_copy(first_hbm, first.at[:, :, :, pl.ds(width, width)], load_sem.at[1]),
+        pltpu.make_async_copy(second_hbm, second, load_sem.at[2]),
+    ]
+    for load in loads:
+        load.start()
+    barrier = pltpu.get_barrier_semaphore()
+    for axis, count, here in (("tm", shards, me), ("dm", bands, band)):
+        for away in range(1, count):
+            peer = lax.rem(here + away, count)
+            pl.semaphore_signal(barrier, inc=1, device_id={axis: peer}, device_id_type=MESH)
+    for piece in range(CHUNKS):
+        row_a = x_ref[pl.ds(2 * piece * step, step, stride=2), :]
+        row_b = x_ref[pl.ds(2 * piece * step + 1, step, stride=2), :]
+        outgoing[piece * step : (piece + 1) * step, :] = jnp.where(chip == 0, row_b, row_a)
+        gathered[me, piece * step : (piece + 1) * step, :] = jnp.where(chip == 0, row_a, row_b)
+    diagonal_ids = lax.broadcasted_iota(jnp.int32, (slots, slots), 0)
+    lane_slots = lax.broadcasted_iota(jnp.int32, (slots, slots), 1)
+    for target in range(bands):
+        line = jnp.where(
+            lane_slots[0:1] < count_ref[0:1, target : target + 1], start_ref[target : target + 1, :], -1
+        ).astype(jnp.float32)
+        column = jnp.sum(jnp.where(diagonal_ids == lane_slots, line, 0.0), axis=1, keepdims=True)
+        marks_out[target] = jnp.broadcast_to(column, (slots, LANES)).astype(jnp.int32)
+    pl.semaphore_wait(barrier, shards + bands - 2)
+
+    def remote(src, dst, sems, index, axis, peer):
+        return pltpu.make_async_remote_copy(
+            src_ref=src, dst_ref=dst, send_sem=sems[0].at[index], recv_sem=sems[1].at[index],
+            device_id={axis: peer}, device_id_type=MESH,
+        )
+
+    row_sems, hop_sems = (send_sem, recv_sem), (hop_send, hop_recv)
+    crossing = []
+    for piece in range(CHUNKS):
+        rows = pl.ds(piece * step, step)
+        crossing.append(remote(outgoing.at[rows], gathered.at[me, rows], row_sems, 1 + piece, "tm", across))
+        crossing[-1].start()
+    own = remote(gathered.at[me], gathered.at[me], row_sems, 0, "tm", sibling)
+    own.start()
+    mark_hop, part_hop, top_hop = [], [], []
+    for away in range(1, bands):
+        peer = lax.rem(band + away, bands)
+        mark_hop.append(remote(marks_out.at[peer], marks.at[band], hop_sems, shards + away, "dm", peer))
+        mark_hop[-1].start()
+
+    odd_core = core == 1
+    shifted = (jnp.where(odd_core, shift_ref[0, 0:1], 1.0), jnp.where(odd_core, shift_ref[1, 0:1], 0.0))
+    corner = 2.0 * math.pi * LANES * res / NT
+    bent = (jnp.where(odd_core, math.cos(corner), 1.0), jnp.where(odd_core, math.sin(corner), 0.0))
+    running = turned((twists_ref[0, 0], twists_ref[0, 1]), shifted)
+    advance = turned((twists_ref[1, 0], twists_ref[1, 1]), bent)
+    for group in range(groups):
+        cols = slice(group * LANES, (group + 1) * LANES)
+        twist_tab[0, :, cols], twist_tab[1, :, cols] = running
+        if group + 1 < groups:
+            running = turned(running, advance)
+
+    for load in loads:
+        load.wait()
+    parity = lax.broadcasted_iota(jnp.int32, (piece_rows, LANES), 0) % 2
+    sign = jnp.where(jnp.logical_and(parity == 1, odd_core), -1.0, 1.0)
+
+    def accumulate(side, piece, fresh):
+        for group in range(groups):
+            cols = slice(group * LANES, (group + 1) * LANES)
+            for half in range(2):
+                taken = gathered[2 * side + half, pl.ds(piece * step + group, piece_rows, stride=groups), :]
+                pair = split_pair(taken * sign)
+                for part in range(2):
+                    base = (4 * part + 2 * half) * piece_rows
+                    x_tab[base : base + piece_rows, cols] = pair[part]
+                    x_tab[base + piece_rows : base + 2 * piece_rows, cols] = pair[part]
+        for block in range(inner // 256):
+            cols = slice(block * 256, (block + 1) * 256)
+            term = jnp.dot(first[side, piece], x_tab[:, cols], preferred_element_type=jnp.float32)
+            partial[:, cols] = term if fresh else partial[:, cols] + term
+
+    own.wait_recv()
+    for piece in range(CHUNKS):
+        accumulate(chip, piece, piece == 0)
+
+    lane_ids = lax.broadcasted_iota(jnp.int32, (res, res), 1)
+    res_ids = lax.broadcasted_iota(jnp.int32, (res, res), 0) + core * res
+    plan = []
+    slot = 0
+    for harmonic in range(1, HARM + 1):
+        depth = (harmonic + 1) // 2
+        plan.append((harmonic, depth, slot))
+        for tile in range(2):
+            target = (lane_ids + tile * res) * harmonic - res_ids
+            for index in range(depth):
+                cycle = index if tile == 0 else harmonic - depth + index
+                hit = jnp.where(target == cycle * N1, 1.0, 0.0)
+                select[tile, (slot + index) * res : (slot + index + 1) * res, :] = hit.astype(jnp.bfloat16)
+        slot += depth
+
+    forwards = []
+    for piece in range(CHUNKS):
+        rows = pl.ds(piece * step, step)
+        crossing[piece].wait_recv()
+        forwards.append(
+            remote(gathered.at[across, rows], gathered.at[across, rows], row_sems, 1 + CHUNKS + piece, "tm", sibling)
+        )
+        forwards[-1].start()
+        if piece > 0:
+            forwards[piece - 1].wait_recv()
+            accumulate(1 - chip, piece - 1, False)
+    forwards[-1].wait_recv()
+    accumulate(1 - chip, CHUNKS - 1, False)
+
+    quarter = inner // 4
+
+    def twisted(block):
+        cols = slice(block * LANES, (block + 1) * LANES)
+        return twist(
+            partial[0:res, cols], partial[res : 2 * res, cols], twist_tab[0, :, cols], twist_tab[1, :, cols]
+        )
+
+    for block in range(quarter // LANES):
+        quads = [twisted(block + turn * (quarter // LANES)) for turn in range(4)]
+        even_re, even_im = quads[0][0] + quads[2][0], quads[0][1] + quads[2][1]
+        odd_re, odd_im = quads[1][0] + quads[3][0], quads[1][1] + quads[3][1]
+        gap_re, gap_im = quads[0][0] - quads[2][0], quads[0][1] - quads[2][1]
+        lag_re, lag_im = quads[1][0] - quads[3][0], quads[1][1] - quads[3][1]
+        cols = slice(block * LANES, (block + 1) * LANES)
+        for kind, value in enumerate(
+            (
+                (even_re + odd_re, even_im + odd_im),
+                (gap_re + lag_im, gap_im - lag_re),
+                (even_re - odd_re, even_im - odd_im),
+                (gap_re - lag_im, gap_im + lag_re),
+            )
+        ):
+            for part in range(2):
+                rows = slice(part * res, (part + 1) * res)
+                b_high[kind, rows, cols], b_low[kind, rows, cols] = split_pair(value[part])
+
+    def against(table, right):
+        return lax.dot_general(table, right, (((1,), (1,)), ((), ())), preferred_element_type=jnp.float32)
+
+    fourth = kept // 4
+    total = jnp.zeros((1, 1), jnp.float32)
+    for kind in range(4):
+        both = against(second[kind], b_high[kind])
+        less = against(second[kind, 0 : 2 * fourth], b_low[kind])
+        by_cos = both[0:fourth] + both[2 * fourth : 3 * fourth] + less[0:fourth]
+        by_sin = both[fourth : 2 * fourth] + both[3 * fourth :] + less[fourth:]
+        x_re = by_cos[:, 0:res] + by_sin[:, res:]
+        x_im = by_cos[:, res:] - by_sin[:, 0:res]
+        bins = (x_re * x_re + x_im * x_im) / NT
+        total = total + jnp.sum(jnp.sum(bins, axis=0, keepdims=True), axis=1, keepdims=True)
+        for column in range(res // LANES):
+            power[column, pl.ds(kind, fourth, stride=4), :] = bins[:, column * LANES : (column + 1) * LANES]
+
+    cycles = NT // (2 * HARM) // N1
+    sums = [jnp.zeros((2 * cycles, res), jnp.float32) for tile in range(2)]
+    slot = 0
+    for harmonic, depth, base in plan:
+        for cycle in range(harmonic):
+            for column in range(res // LANES):
+                high, low = split_pair(power[column, pl.ds(cycle, cycles, stride=harmonic), :])
+                cols = slice((slot + cycle) * res + column * LANES, (slot + cycle) * res + (column + 1) * LANES)
+                picks[0:cycles, cols] = high
+                picks[cycles : 2 * cycles, cols] = low
+        for tile in range(2):
+            begin = (slot + (0 if tile == 0 else harmonic - depth)) * res
+            sums[tile] = sums[tile] + jnp.dot(
+                picks[:, begin : begin + depth * res],
+                select[tile, base * res : (base + depth) * res, :],
+                preferred_element_type=jnp.float32,
+            )
+        slot += harmonic
+    mean = total / (kept * res)
+    off = power[...] - mean[None]
+    deviation = jnp.sum(jnp.sum(jnp.sum(off * off, axis=0), axis=0, keepdims=True), axis=1, keepdims=True)
+    mean = jnp.broadcast_to(mean, (8, LANES))
+    deviation = jnp.broadcast_to(deviation, (8, LANES))
+    each, lead = cycles // shards, N1 // LANES
+    base = lead * each
+    for shard in range(shards):
+        for column in range(lead):
+            found = sums[column * LANES // res][:, column * LANES % res : column * LANES % res + LANES]
+            mine[shard, column * each : (column + 1) * each, :] = (
+                found[shard * each : (shard + 1) * each] + found[cycles + shard * each : cycles + (shard + 1) * each]
+            )
+        mine[shard, base : base + 8, :] = mean
+        mine[shard, base + 8 : base + 16, :] = deviation
+    for away in range(1, shards):
+        peer = lax.rem(me + away, shards)
+        part_hop.append(remote(mine.at[peer], parts.at[me], hop_sems, away, "tm", peer))
+        part_hop[-1].start()
+    parts[me] = mine[me]
+    marks[band] = marks_out[band]
+    for copy in part_hop:
+        copy.wait_recv()
+
+    bin_total = NT // 2
+    share = bin_total // 2
+    found = []
+    for row in range(2):
+        left, right = parts[2 * row], parts[2 * row + 1]
+        mean_l, mean_r = left[base : base + 8], right[base : base + 8]
+        row_mean = 0.5 * (mean_l + mean_r)
+        gap_l, gap_r = mean_l - row_mean, mean_r - row_mean
+        squares = left[base + 8 : base + 16] + right[base + 8 : base + 16]
+        spread = (squares + share * (gap_l * gap_l + gap_r * gap_r)) / bin_total
+        scale = jnp.sqrt(spread + EPSILON)
+        found.append((left[:base] + right[:base] - HARM * row_mean[0:1]) / scale[0:1])
+    highest = jnp.maximum(found[0], found[1])
+    level = (found[0] + found[1]) / 2
+    for column in range(lead):
+        block = slice(column * each, (column + 1) * each)
+        flat_top[pl.ds(column, each, stride=lead), :] = highest[block]
+        flat_level[pl.ds(column, each, stride=lead), :] = level[block]
+        for row in range(2):
+            harm_ref[pl.ds(2 * column + row, each, stride=2 * lead), :] = found[row][block]
+    sent = jnp.maximum(marks_out[...].reshape(bands * slots, LANES), 0)
+    tops_out[...] = windows(flat_top[...], sent).reshape(bands, slots, LANES)
+    for away in range(1, bands):
+        peer = lax.rem(band + away, bands)
+        top_hop.append(remote(tops_out.at[peer], tops.at[band], hop_sems, shards + bands + away, "dm", peer))
+        top_hop[-1].start()
+    tops[band] = tops_out[band]
+    for copy in mark_hop:
+        copy.wait_recv()
+    wanted = marks[...].reshape(bands * slots, LANES)
+    floor = windows(flat_level[...], jnp.maximum(wanted, 0)).reshape(bands, slots, LANES)
+    for copy in top_hop:
+        copy.wait_recv()
+    sift_ref[...] = jnp.where(marks[...] >= 0, tops[...] - floor, 0.0)
+    own.wait_send()
+    for copy in crossing + forwards + mark_hop + part_hop + top_hop:
+        copy.wait_send()
+
+
+def fast_device(tables, series, cand_start, cand_count):
+    first, twists, shift, second = tables
+    dm_rows, samples_dev = series.shape
+    shards, bands = lax.axis_size("tm"), lax.axis_size("dm")
+    inner, res = NT // N1, N1 // 2
+    kept = inner // 2
+    size = samples_dev // LANES
+    cycles = NT // (2 * HARM) // N1
+    each, lead = cycles // shards, N1 // LANES
+    steps = HARM * (HARM + 1) // 2
+    depth = sum((harmonic + 1) // 2 for harmonic in range(1, HARM + 1))
+    slots = cand_start.shape[3]
+    blocks = lead * each
+    width = blocks + 16
+    vmem, anywhere = pl.BlockSpec(memory_space=pltpu.VMEM), pl.BlockSpec(memory_space=pl.ANY)
+    lined = series.reshape(dm_rows, size, LANES).swapaxes(0, 1).reshape(size * dm_rows, LANES)
+    low, wide = jnp.bfloat16, jnp.float32
+    harm, sifted = pl.pallas_call(
+        search_kernel,
+        out_shape=(
+            jax.ShapeDtypeStruct((dm_rows * blocks, LANES), wide),
+            jax.ShapeDtypeStruct((bands, slots, LANES), wide),
+        ),
+        in_specs=[vmem, vmem, vmem, anywhere, vmem, vmem, anywhere],
+        out_specs=(vmem, vmem),
+        scratch_shapes=[
+            pltpu.VMEM((shards, size, LANES), wide),
+            pltpu.VMEM((size, LANES), wide),
+            pltpu.VMEM((2 * first.shape[3], inner), low),
+            pltpu.VMEM(first.shape[:3] + (2 * first.shape[3],), low),
+            pltpu.VMEM((2, res, inner), wide),
+            pltpu.VMEM(second.shape, low),
+            pltpu.VMEM((2 * res, inner), wide),
+            pltpu.VMEM((4, 2 * res, inner // 4), low),
+            pltpu.VMEM((4, 2 * res, inner // 4), low),
+            pltpu.VMEM((res // LANES, kept, LANES), wide),
+            pltpu.VMEM((2 * cycles, steps * res), low),
+            pltpu.VMEM((2, depth * res, res), low),
+            pltpu.VMEM((shards, width, LANES), wide),
+            pltpu.VMEM((shards, width, LANES), wide),
+            pltpu.VMEM((bands, slots, LANES), jnp.int32),
+            pltpu.VMEM((bands, slots, LANES), jnp.int32),
+            pltpu.VMEM((bands, slots, LANES), wide),
+            pltpu.VMEM((bands, slots, LANES), wide),
+            pltpu.VMEM((blocks, LANES), wide),
+            pltpu.VMEM((blocks, LANES), wide),
+            pltpu.SemaphoreType.DMA((3,)),
+            pltpu.SemaphoreType.DMA((1 + 2 * CHUNKS,)),
+            pltpu.SemaphoreType.DMA((1 + 2 * CHUNKS,)),
+            pltpu.SemaphoreType.DMA((shards + 2 * bands,)),
+            pltpu.SemaphoreType.DMA((shards + 2 * bands,)),
+        ],
+        compiler_params=pltpu.CompilerParams(
+            collective_id=0, has_side_effects=True, vmem_limit_bytes=VMEM_LIMIT
+        ),
+    )(
+        lined, cand_start[0, 0], cand_count[0], jnp.asarray(first), jnp.asarray(twists), jnp.asarray(shift),
+        jnp.asarray(second),
+    )
+    harmonic_sum = harm.reshape(blocks, dm_rows, LANES).swapaxes(0, 1).reshape(dm_rows, blocks * LANES)
+    return (harmonic_sum, sifted[None, None])
+
+
+def fits(mesh):
+    return mesh.shape["tm"] == 4 and BW == LANES
+
+
 def solution(mesh):
+    if fits(mesh):
+        tables = dft_tables(mesh.shape["tm"])
+
+        def body(series, cand_start, cand_count):
+            if series.shape[0] != 2:
+                return per_device(series, cand_start, cand_count)
+            return fast_device(tables, series, cand_start, cand_count)
+    else:
+        body = per_device
     return jax.shard_map(
-        per_device,
+        body,
         mesh=mesh,
         in_specs=(
             P(("beam", "dm"), "tm"),

time: 822 us -> 34.6 us (0.04); the launches traced: 811 us -> 34.5 us
  local copies, waits for them, and re-layouts: 458 us -> 2.1 us
  waiting for transfers between devices: 148 us -> 0 us
  other arithmetic: 104 us -> 0 us
  matrix products: 52.8 us -> 0 us
  Pallas kernels: 0 us -> 31.7 us
  starting transfers between devices: 21.9 us -> 0 us
  between operations: 14.9 us -> 0.65 us
  blocking collectives: 11.4 us -> 0 us
    gather x11 -> x0, local copies, waits for them, and re-layouts: 385 us -> none  [the longest x8 307 us: per_device(): jnp.take(score_flat, flat_index.reshape(-1), axis=1)]
    reduce_scatter x1 -> x0, waiting for transfers between devices: 126 us -> none  [per_device(): summed = lax.psum_scatter(dense.T, 'tm', scatter_dimension=0, tiled=True)]
    select_n x13 -> x0, other arithmetic: 62.3 us -> none  [the longest x8 60.3 us: per_device(): jnp.take(score_flat, flat_index.reshape(-1), axis=1)]
    reshape x12 -> x0, local copies, waits for them, and re-layouts: 57.6 us -> none  [the longest x8 29.9 us: per_device(): jnp.take(score_flat, flat_index.reshape(-1), axis=1)]
    dot_general x6 -> x0, matrix products: 52.8 us -> none  [contract(): return jnp.einsum(pattern, left, right, precision=lax.Precision.HIGHEST)]
    scatter-add x1 -> x0, other arithmetic: 32.8 us -> none  [per_device(): jnp.zeros((dm_rows, cycles, N1), jnp.float32).at[:, :, my_residues]]
    pallas_call x0 -> x1, Pallas kernels: none -> 31.7 us  [fast_device(): pl.pallas_call(search_kernel, out_shape=(jax.ShapeDtypeStruct((dm_rows *...]
    all_to_all x5 -> x0, starting transfers between devices: 21.5 us -> none  [the longest x1 5.6 us: per_device(): lax.all_to_all(markers, 'dm', split_axis=0, concat_axis=0, tiled=True)]
  transfers between devices with their start and end apart: 6 -> 0, of which waited for: 4 -> 0; matrix products, arithmetic and copies ran while one was open for 13% -> 0% of each run, Pallas kernels for 0% -> 0%
where the time goes in v2:
time: 34.6 us; the launch traced here: 34.5 us
  Pallas kernels  31.7 us (92%)
  local copies, waits for them, and re-layouts  2.1 us (6%)
  between operations  0.65 us (2%)
    pallas_call x1, Pallas kernels, fast_device(): pl.pallas_call(search_kernel, out_shape=(jax.ShapeDtypeStruct((dm_rows *...  31.7 us
    unnamed x4, local copies, waits for them, and re-layouts  2.1 us

profile of v2, /device:TPU:0, one launch (start us, length us, event | category | flops | bytes accessed | tf_op | source)
XLA Modules:
  0.0 34.5 jit_solution(6492555393707015143)
XLA Ops:
  0.6 31.7 %shard_map.86 = (f32[128,128]{1,0:T(8,128)}, f32[4,16,128]{2,1,0:T(8,128)}) custom-call(f32[2048,128]{1,0:T(8,128)} %bitcast.13, s32[4,16]{1,0:T(4,128)} %bitcast.16, s32[1,4]{1,0:T(1,128)} %bitcast.17, bf16[2,4,512,128]{3,2,1,0:T(8,128)(2,1)} %constant.8.clone.first_hbm, f32[2,2,256,128]{3,2,1,0:T(8,128)} %constant.9.clone.twists_ref, ...), custom_call_target="tpu_custom_call" | custom-call | tf_op jit(solution)/shard_map/pallas_call | solution.py:494
  32.3 0.0 copy-start
  32.4 1.5 %copy.13 = f32[2,8192]{1,0:T(2,128)} copy(f32[2,8192]{1,0:T(2,128)} %bitcast.14) | data formatting | bytes 131072
  33.8 0.0 copy-done
  33.8 0.6 %copy.14 = f32[1,1,4,16,128]{4,3,2,1,0:T(8,128)} copy(f32[1,1,4,16,128]{4,3,2,1,0:T(8,128)S(1)} %bitcast.15) | data formatting | bytes 65536
Async XLA Ops:
  32.3 1.5 %copy-start = (f32[4,16,128]{2,1,0:T(8,128)S(1)}, f32[4,16,128]{2,1,0:T(8,128)}, u32[]{:S(2)}) copy-start(f32[4,16,128]{2,1,0:T(8,128)} %get-tuple-element.5) | copy-start | bytes 98308

commit v3 on v2

--- a/solution.py
+++ b/solution.py
@@ -217,8 +217,8 @@
 
 
 def search_kernel(
-    x_ref, start_ref, count_ref, first_hbm, twists_ref, shift_ref, second_hbm, harm_ref, sift_ref,
-    gathered, outgoing, x_tab, first, twist_tab, second, partial, b_high, b_low, power, picks, select,
+    x_hbm, start_ref, count_ref, first_hbm, twists_ref, shift_ref, second_hbm, harm_ref, scale_ref, sift_ref,
+    x_ref, gathered, outgoing, x_tab, first, twist_tab, second, partial, b_high, b_low, power, picks, select,
     mine, parts, marks_out, marks, tops_out, tops, flat_top, flat_level,
     load_sem, send_sem, recv_sem, hop_send, hop_recv,
 ):
@@ -236,6 +236,16 @@
     kept = power.shape[1]
     slots = sift_ref.shape[1]
 
+    barrier = pltpu.get_barrier_semaphore()
+    for axis, count, here in (("tm", shards, me), ("dm", bands, band)):
+        for away in range(1, count):
+            peer = lax.rem(here + away, count)
+            pl.semaphore_signal(barrier, inc=1, device_id={axis: peer}, device_id_type=MESH)
+    arrivals = []
+    for piece in range(CHUNKS):
+        rows = pl.ds(2 * piece * step, 2 * step)
+        arrivals.append(pltpu.make_async_copy(x_hbm.at[rows], x_ref.at[rows], load_sem.at[3 + piece]))
+        arrivals[-1].start()
     width = first_hbm.shape[3]
     loads = [
         pltpu.make_async_copy(first_hbm, first.at[:, :, :, pl.ds(0, width)], load_sem.at[0]),
@@ -244,12 +254,8 @@
     ]
     for load in loads:
         load.start()
-    barrier = pltpu.get_barrier_semaphore()
-    for axis, count, here in (("tm", shards, me), ("dm", bands, band)):
-        for away in range(1, count):
-            peer = lax.rem(here + away, count)
-            pl.semaphore_signal(barrier, inc=1, device_id={axis: peer}, device_id_type=MESH)
     for piece in range(CHUNKS):
+        arrivals[piece].wait()
         row_a = x_ref[pl.ds(2 * piece * step, step, stride=2), :]
         row_b = x_ref[pl.ds(2 * piece * step + 1, step, stride=2), :]
         outgoing[piece * step : (piece + 1) * step, :] = jnp.where(chip == 0, row_b, row_a)
@@ -301,9 +307,15 @@
     parity = lax.broadcasted_iota(jnp.int32, (piece_rows, LANES), 0) % 2
     sign = jnp.where(jnp.logical_and(parity == 1, odd_core), -1.0, 1.0)
 
-    def accumulate(side, piece, fresh):
+    quads = groups // 4
+
+    def place(group):
+        spot = group % quads * 4 + group // quads
+        return slice(spot * LANES, (spot + 1) * LANES)
+
+    def prepare(side, piece):
         for group in range(groups):
-            cols = slice(group * LANES, (group + 1) * LANES)
+            cols = place(group)
             for half in range(2):
                 taken = gathered[2 * side + half, pl.ds(piece * step + group, piece_rows, stride=groups), :]
                 pair = split_pair(taken * sign)
@@ -311,10 +323,16 @@
                     base = (4 * part + 2 * half) * piece_rows
                     x_tab[base : base + piece_rows, cols] = pair[part]
                     x_tab[base + piece_rows : base + 2 * piece_rows, cols] = pair[part]
-        for block in range(inner // 256):
+
+    def multiply(side, piece, fresh, spans):
+        for block in spans:
             cols = slice(block * 256, (block + 1) * 256)
             term = jnp.dot(first[side, piece], x_tab[:, cols], preferred_element_type=jnp.float32)
             partial[:, cols] = term if fresh else partial[:, cols] + term
+
+    def accumulate(side, piece, fresh):
+        prepare(side, piece)
+        multiply(side, piece, fresh, range(inner // 256))
 
     own.wait_recv()
     for piece in range(CHUNKS):
@@ -347,22 +365,23 @@
             forwards[piece - 1].wait_recv()
             accumulate(1 - chip, piece - 1, False)
     forwards[-1].wait_recv()
-    accumulate(1 - chip, CHUNKS - 1, False)
+    prepare(1 - chip, CHUNKS - 1)
 
     quarter = inner // 4
 
     def twisted(block):
-        cols = slice(block * LANES, (block + 1) * LANES)
+        cols, spot = slice(block * LANES, (block + 1) * LANES), place(block)
         return twist(
-            partial[0:res, cols], partial[res : 2 * res, cols], twist_tab[0, :, cols], twist_tab[1, :, cols]
+            partial[0:res, spot], partial[res : 2 * res, spot], twist_tab[0, :, cols], twist_tab[1, :, cols]
         )
 
     for block in range(quarter // LANES):
-        quads = [twisted(block + turn * (quarter // LANES)) for turn in range(4)]
-        even_re, even_im = quads[0][0] + quads[2][0], quads[0][1] + quads[2][1]
-        odd_re, odd_im = quads[1][0] + quads[3][0], quads[1][1] + quads[3][1]
-        gap_re, gap_im = quads[0][0] - quads[2][0], quads[0][1] - quads[2][1]
-        lag_re, lag_im = quads[1][0] - quads[3][0], quads[1][1] - quads[3][1]
+        multiply(1 - chip, CHUNKS - 1, False, range(2 * block, 2 * block + 2))
+        four = [twisted(block + turn * (quarter // LANES)) for turn in range(4)]
+        even_re, even_im = four[0][0] + four[2][0], four[0][1] + four[2][1]
+        odd_re, odd_im = four[1][0] + four[3][0], four[1][1] + four[3][1]
+        gap_re, gap_im = four[0][0] - four[2][0], four[0][1] - four[2][1]
+        lag_re, lag_im = four[1][0] - four[3][0], four[1][1] - four[3][1]
         cols = slice(block * LANES, (block + 1) * LANES)
         for kind, value in enumerate(
             (
@@ -414,8 +433,8 @@
     mean = total / (kept * res)
     off = power[...] - mean[None]
     deviation = jnp.sum(jnp.sum(jnp.sum(off * off, axis=0), axis=0, keepdims=True), axis=1, keepdims=True)
-    mean = jnp.broadcast_to(mean, (8, LANES))
-    deviation = jnp.broadcast_to(deviation, (8, LANES))
+    stat_rows = lax.broadcasted_iota(jnp.int32, (8, LANES), 0)
+    stats = jnp.where(stat_rows == 0, mean, deviation)
     each, lead = cycles // shards, N1 // LANES
     base = lead * each
     for shard in range(shards):
@@ -424,8 +443,7 @@
             mine[shard, column * each : (column + 1) * each, :] = (
                 found[shard * each : (shard + 1) * each] + found[cycles + shard * each : cycles + (shard + 1) * each]
             )
-        mine[shard, base : base + 8, :] = mean
-        mine[shard, base + 8 : base + 16, :] = deviation
+        mine[shard, base : base + 8, :] = stats
     for away in range(1, shards):
         peer = lax.rem(me + away, shards)
         part_hop.append(remote(mine.at[peer], parts.at[me], hop_sems, away, "tm", peer))
@@ -437,24 +455,27 @@
 
     bin_total = NT // 2
     share = bin_total // 2
-    found = []
+    found, raw, scales = [], [], []
     for row in range(2):
         left, right = parts[2 * row], parts[2 * row + 1]
-        mean_l, mean_r = left[base : base + 8], right[base : base + 8]
+        mean_l, mean_r = left[base : base + 1], right[base : base + 1]
         row_mean = 0.5 * (mean_l + mean_r)
         gap_l, gap_r = mean_l - row_mean, mean_r - row_mean
-        squares = left[base + 8 : base + 16] + right[base + 8 : base + 16]
+        squares = left[base + 1 : base + 2] + right[base + 1 : base + 2]
         spread = (squares + share * (gap_l * gap_l + gap_r * gap_r)) / bin_total
-        scale = jnp.sqrt(spread + EPSILON)
-        found.append((left[:base] + right[:base] - HARM * row_mean[0:1]) / scale[0:1])
+        scales.append(jnp.sqrt(spread + EPSILON))
+        raw.append(left[:base] + right[:base] - HARM * row_mean)
+        found.append(raw[row] / scales[row])
     highest = jnp.maximum(found[0], found[1])
     level = (found[0] + found[1]) / 2
+    odd_rows = lax.broadcasted_iota(jnp.int32, (8, LANES), 0) % 2 == 1
+    scale_ref[...] = jnp.where(odd_rows, scales[1], scales[0])
     for column in range(lead):
         block = slice(column * each, (column + 1) * each)
         flat_top[pl.ds(column, each, stride=lead), :] = highest[block]
         flat_level[pl.ds(column, each, stride=lead), :] = level[block]
         for row in range(2):
-            harm_ref[pl.ds(2 * column + row, each, stride=2 * lead), :] = found[row][block]
+            harm_ref[pl.ds(2 * column + row, each, stride=2 * lead), :] = raw[row][block]
     sent = jnp.maximum(marks_out[...].reshape(bands * slots, LANES), 0)
     tops_out[...] = windows(flat_top[...], sent).reshape(bands, slots, LANES)
     for away in range(1, bands):
@@ -487,19 +508,21 @@
     depth = sum((harmonic + 1) // 2 for harmonic in range(1, HARM + 1))
     slots = cand_start.shape[3]
     blocks = lead * each
-    width = blocks + 16
+    width = blocks + 8
     vmem, anywhere = pl.BlockSpec(memory_space=pltpu.VMEM), pl.BlockSpec(memory_space=pl.ANY)
     lined = series.reshape(dm_rows, size, LANES).swapaxes(0, 1).reshape(size * dm_rows, LANES)
     low, wide = jnp.bfloat16, jnp.float32
-    harm, sifted = pl.pallas_call(
+    harm, scale, sifted = pl.pallas_call(
         search_kernel,
         out_shape=(
             jax.ShapeDtypeStruct((dm_rows * blocks, LANES), wide),
+            jax.ShapeDtypeStruct((8, LANES), wide),
             jax.ShapeDtypeStruct((bands, slots, LANES), wide),
         ),
-        in_specs=[vmem, vmem, vmem, anywhere, vmem, vmem, anywhere],
-        out_specs=(vmem, vmem),
+        in_specs=[anywhere, vmem, vmem, anywhere, vmem, vmem, anywhere],
+        out_specs=(vmem, vmem, vmem),
         scratch_shapes=[
+            pltpu.VMEM((dm_rows * size, LANES), wide),
             pltpu.VMEM((shards, size, LANES), wide),
             pltpu.VMEM((size, LANES), wide),
             pltpu.VMEM((2 * first.shape[3], inner), low),
@@ -520,7 +543,7 @@
             pltpu.VMEM((bands, slots, LANES), wide),
             pltpu.VMEM((blocks, LANES), wide),
             pltpu.VMEM((blocks, LANES), wide),
-            pltpu.SemaphoreType.DMA((3,)),
+            pltpu.SemaphoreType.DMA((3 + CHUNKS,)),
             pltpu.SemaphoreType.DMA((1 + 2 * CHUNKS,)),
             pltpu.SemaphoreType.DMA((1 + 2 * CHUNKS,)),
             pltpu.SemaphoreType.DMA((shards + 2 * bands,)),
@@ -533,6 +556,7 @@
         lined, cand_start[0, 0], cand_count[0], jnp.asarray(first), jnp.asarray(twists), jnp.asarray(shift),
         jnp.asarray(second),
     )
+    harm = (harm.reshape(-1, 8, LANES) / scale[None]).reshape(harm.shape)
     harmonic_sum = harm.reshape(blocks, dm_rows, LANES).swapaxes(0, 1).reshape(dm_rows, blocks * LANES)
     return (harmonic_sum, sifted[None, None])
 

time: 34.6 us -> 34.4 us (level)
  other arithmetic: 0 us -> 0.67 us
  local copies, waits for them, and re-layouts: 2.1 us -> 1.53 us
  Pallas kernels: 31.7 us -> 31.3 us
    unnamed x4 -> x5, local copies, waits for them, and re-layouts: 2.1 us -> 0.81 us
    div x0 -> x1, local copies, waits for them, and re-layouts: none -> 0.72 us  [fast_device(): harm = (harm.reshape(-1, 8, LANES) / scale[None]).reshape(harm.shape)]
    reshape x0 -> x1, other arithmetic: none -> 0.67 us  [fast_device(): harm.reshape(blocks, dm_rows, LANES).swapaxes(0, 1)]
    pallas_call x1, Pallas kernels: 31.7 us -> 31.3 us  [fast_device(): pl.pallas_call(search_kernel, out_shape=(jax.ShapeDtypeStruct((dm_rows *...]
where the time goes in v3:
time: 34.4 us; the launch traced here: 34.1 us
  Pallas kernels  31.3 us (91%)
  local copies, waits for them, and re-layouts  1.53 us (4%)
  other arithmetic  0.67 us (2%)
  between operations  0.65 us (2%)
    pallas_call x1, Pallas kernels, fast_device(): pl.pallas_call(search_kernel, out_shape=(jax.ShapeDtypeStruct((dm_rows *...  31.3 us
    unnamed x5, local copies, waits for them, and re-layouts  0.81 us
    div x1, local copies, waits for them, and re-layouts, fast_device(): harm = (harm.reshape(-1, 8, LANES) / scale[None]).reshape(harm.shape)  0.72 us

profile of v3, /device:TPU:0, one launch (start us, length us, event | category | flops | bytes accessed | tf_op | source)
XLA Modules:
  0.0 34.1 jit_solution(13773809580668173728)
XLA Ops:
  0.6 31.3 %shard_map.86 = (f32[128,128]{1,0:T(8,128)}, f32[8,128]{1,0:T(8,128)}, f32[4,16,128]{2,1,0:T(8,128)}) custom-call(f32[2048,128]{1,0:T(8,128)} %bitcast.14, s32[4,16]{1,0:T(4,128)} %bitcast.18, s32[1,4]{1,0:T(1,128)} %bitcast.19, bf16[2,4,512,128]{3,2,1,0:T(8,128)(2,1)} %constant.8.clone.first_hbm, f32[2,2,256,128]{3,2,1,0:T(8,128)} %constant.9.clone.twists_ref, ...), custom_call_target="tpu_custom_call" | custom-call | tf_op jit(solution)/shard_map/pallas_call | solution.py:515
  31.9 0.0 copy-start
  31.9 0.7 %div.11 = f32[16,8,128]{2,1,0:T(8,128)S(1)} broadcast(f32[8,128]{1,0:T(8,128)} %get-tuple-element.6), dimensions={1,2} | broadcast | bytes 69632 | tf_op jit(solution)/shard_map/div | solution.py:559
  32.7 0.1 copy-done
  32.8 0.0 copy-start.1
  32.8 0.7 %divide_bitcast_fusion = f32[2,8192]{1,0:T(2,128)} fusion(f32[64,2,128]{2,1,0:T(2,128)S(1)} %bitcast.16, f32[64,2,128]{2,1,0:T(2,128)S(1)} %bitcast.15), kind=kLoop, calls=%fused_computation | loop fusion | flops 16384 | bytes 196608 | tf_op jit(solution)/shard_map/reshape | solution.py:560
  33.4 0.1 copy-done.1
  33.5 0.6 %copy.12 = f32[1,1,4,16,128]{4,3,2,1,0:T(8,128)} copy(f32[1,1,4,16,128]{4,3,2,1,0:T(8,128)S(1)} %bitcast.17) | data formatting | bytes 65536
Async XLA Ops:
  31.9 0.8 %copy-start = (f32[128,128]{1,0:T(8,128)S(1)}, f32[128,128]{1,0:T(8,128)}, u32[]{:S(2)}) copy-start(f32[128,128]{1,0:T(8,128)} %get-tuple-element.5) | copy-start | bytes 196612
  32.8 0.8 %copy-start.1 = (f32[4,16,128]{2,1,0:T(8,128)S(1)}, f32[4,16,128]{2,1,0:T(8,128)}, u32[]{:S(2)}) copy-start(f32[4,16,128]{2,1,0:T(8,128)} %get-tuple-element.7) | copy-start | bytes 98308

commit v4 on v3

--- a/solution.py
+++ b/solution.py
@@ -473,15 +473,17 @@
     for column in range(lead):
         block = slice(column * each, (column + 1) * each)
         flat_top[pl.ds(column, each, stride=lead), :] = highest[block]
-        flat_level[pl.ds(column, each, stride=lead), :] = level[block]
-        for row in range(2):
-            harm_ref[pl.ds(2 * column + row, each, stride=2 * lead), :] = raw[row][block]
     sent = jnp.maximum(marks_out[...].reshape(bands * slots, LANES), 0)
     tops_out[...] = windows(flat_top[...], sent).reshape(bands, slots, LANES)
     for away in range(1, bands):
         peer = lax.rem(band + away, bands)
         top_hop.append(remote(tops_out.at[peer], tops.at[band], hop_sems, shards + bands + away, "dm", peer))
         top_hop[-1].start()
+    for column in range(lead):
+        block = slice(column * each, (column + 1) * each)
+        flat_level[pl.ds(column, each, stride=lead), :] = level[block]
+        for row in range(2):
+            harm_ref[pl.ds(2 * column + row, each, stride=2 * lead), :] = raw[row][block]
     tops[band] = tops_out[band]
     for copy in mark_hop:
         copy.wait_recv()
@@ -493,6 +495,14 @@
     own.wait_send()
     for copy in crossing + forwards + mark_hop + part_hop + top_hop:
         copy.wait_send()
+
+
+def finish_kernel(raw_ref, scale_ref, excess_ref, harm_ref, sift_ref):
+    scale = scale_ref[...]
+    for group in range(raw_ref.shape[0] // 8):
+        rows = slice(group * 8, (group + 1) * 8)
+        harm_ref[rows, :] = raw_ref[rows, :] / scale
+    sift_ref[...] = excess_ref[...]
 
 
 def fast_device(tables, series, cand_start, cand_count):
@@ -556,7 +566,15 @@
         lined, cand_start[0, 0], cand_count[0], jnp.asarray(first), jnp.asarray(twists), jnp.asarray(shift),
         jnp.asarray(second),
     )
-    harm = (harm.reshape(-1, 8, LANES) / scale[None]).reshape(harm.shape)
+    harm, sifted = pl.pallas_call(
+        finish_kernel,
+        out_shape=(
+            jax.ShapeDtypeStruct(harm.shape, wide),
+            jax.ShapeDtypeStruct(sifted.shape, wide),
+        ),
+        in_specs=[vmem, vmem, vmem],
+        out_specs=(vmem, vmem),
+    )(harm, scale, sifted)
     harmonic_sum = harm.reshape(blocks, dm_rows, LANES).swapaxes(0, 1).reshape(dm_rows, blocks * LANES)
     return (harmonic_sum, sifted[None, None])
 

time: 34.4 us -> 33.6 us (0.977)
  local copies, waits for them, and re-layouts: 1.53 us -> 0 us
  Pallas kernels: 31.3 us -> 32.8 us
  other arithmetic: 0.67 us -> 0 us
    pallas_call x0 -> x1, Pallas kernels: none -> 1.49 us  [fast_device(): pl.pallas_call(finish_kernel, out_shape=(jax.ShapeDtypeStruct(harm.shape,...]
    unnamed x5 -> x0, local copies, waits for them, and re-layouts: 0.81 us -> none
    div x1 -> x0, local copies, waits for them, and re-layouts: 0.72 us -> none  [fast_device(): harm = (harm.reshape(-1, 8, LANES) / scale[None]).reshape(harm.shape)]
    reshape x1 -> x0, other arithmetic: 0.67 us -> none  [fast_device(): harm.reshape(blocks, dm_rows, LANES).swapaxes(0, 1)]
where the time goes in v4:
time: 33.6 us; the launch traced here: 33.4 us
  Pallas kernels  32.8 us (98%)
  between operations  0.64 us (2%)
    pallas_call x1, Pallas kernels, fast_device(): pl.pallas_call(search_kernel, out_shape=(jax.ShapeDtypeStruct((dm_rows *...  31.3 us
    pallas_call x1, Pallas kernels, fast_device(): pl.pallas_call(finish_kernel, out_shape=(jax.ShapeDtypeStruct(harm.shape,...  1.49 us

profile of v4, /device:TPU:0, one launch (start us, length us, event | category | flops | bytes accessed | tf_op | source)
XLA Modules:
  0.0 33.4 jit_solution(4588162338934171407)
XLA Ops:
  0.6 31.3 %shard_map.86 = (f32[128,128]{1,0:T(8,128)}, f32[8,128]{1,0:T(8,128)}, f32[4,16,128]{2,1,0:T(8,128)}) custom-call(f32[2048,128]{1,0:T(8,128)} %bitcast.13, s32[4,16]{1,0:T(4,128)} %bitcast.14, s32[1,4]{1,0:T(1,128)} %bitcast.15, bf16[2,4,512,128]{3,2,1,0:T(8,128)(2,1)} %constant.8.clone.first_hbm, f32[2,2,256,128]{3,2,1,0:T(8,128)} %constant.9.clone.twists_ref, ...), custom_call_target="tpu_custom_call" | custom-call | tf_op jit(solution)/shard_map/pallas_call | solution.py:525
  31.9 1.5 %shard_map.87 = (f32[128,128]{1,0:T(8,128)}, f32[4,16,128]{2,1,0:T(8,128)}) custom-call(f32[128,128]{1,0:T(8,128)} %get-tuple-element.7.raw_ref, f32[8,128]{1,0:T(8,128)} %get-tuple-element.8.scale_ref, f32[4,16,128]{2,1,0:T(8,128)} %get-tuple-element.9.excess_ref), custom_call_target="tpu_custom_call" | custom-call | tf_op jit(solution)/shard_map/pallas_call | solution.py:569
